TPU v7x, 256 devices: a 2x2x32 block of a 4x8x32 slice. The times are simulated.
256 devices in a mesh: band: 4 (over y, x), row: 64 (over z, core).
Axes of the slice: x: 2, y: 2, z: 32, core: 2. Of those that a mesh axis runs over, the one named last changes fastest.
The devices are a block of a 4x8x32 slice.
Arguments:
- shot_traces: bfloat16 [131072, 4096], P(('band', 'row')), parts along dimension 0, may hold values from -6 to 6
- source_cell: int32 [131072], P(('band', 'row')), parts along dimension 0, may hold values from 0 to 127
- receiver_cell: int32 [131072], P(('band', 'row')), parts along dimension 0, may hold values from 0 to 127
- band_order: int32 [512], P('band'), parts along dimension 0, may hold values from 0 to 127, each once
Outputs:
- next_grid: float32 [512, 2, 128, 128], P(('band', 'row')), parts along dimension 0
There are 4 independent parts, one for each index of `band`. A program takes and returns all parts, laid end to end along the dimension named above; each array names one. Nothing has to cross between parts.
Inputs may be any that keep to these rules, and one draw needn't show every extreme that they name: `band_order`: a permutation of 0 to 127.
All inputs are finite; a program needn't handle non-finite values.
Results may differ from a plain program's by a relative error of at most 0.0037.
Values may be sent and summed in bfloat16 or wider, within the bound.
A program may use at most 64 MiB of HBM per device.

v0:
```python
import math
import jax
import jax.numpy as jnp
from jax import lax
from jax.sharding import PartitionSpec as P

FLO = 64
SC = 128
RC = 128


def local(shot_traces, source_cell, receiver_cell, band_order):
    samples_count = shot_traces.shape[1]
    band_size = band_order.shape[0]
    local_traces = shot_traces.shape[0]
    bins = FLO + band_order
    samples = jnp.arange(samples_count, dtype=jnp.int32)
    phase = samples[:, None] * bins[None, :] % samples_count
    angle = 2.0 * math.pi * phase.astype(jnp.float32) / samples_count
    scale = 1.0 / math.sqrt(samples_count)
    table = jnp.concatenate([jnp.cos(angle) * scale, -jnp.sin(angle) * scale], axis=1).astype(
        jnp.bfloat16
    )
    spectra = jnp.dot(shot_traces, table, preferred_element_type=jnp.float32).astype(jnp.bfloat16)
    spectra = spectra.reshape(local_traces, 2, band_size)
    source_range = jnp.arange(SC, dtype=jnp.float32)
    receiver_range = jnp.arange(RC, dtype=jnp.float32)
    cells = jnp.stack([source_cell, receiver_cell], axis=1).astype(jnp.bfloat16)
    cells = jnp.broadcast_to(cells[:, :, None], (local_traces, 2, band_size))
    packed = jnp.concatenate([spectra, cells], axis=1)
    moved = lax.all_to_all(packed, "row", split_axis=2, concat_axis=0, tiled=True)
    received = moved[:, 0:2, :]
    source_value = moved[:, 2, 0].astype(jnp.float32)
    receiver_value = moved[:, 3, 0].astype(jnp.float32)
    source_hot = (source_value[:, None] == source_range[None, :]).astype(jnp.bfloat16)
    receiver_hot = (receiver_value[:, None] == receiver_range[None, :]).astype(jnp.bfloat16)
    counts = jnp.einsum("ts,tr->sr", source_hot, receiver_hot, preferred_element_type=jnp.float32)
    weighted = received[:, :, :, None] * receiver_hot[:, None, None, :]
    stack = jnp.einsum("ts,tcfr->fcsr", source_hot, weighted, preferred_element_type=jnp.float32)
    next_grid = stack / jnp.maximum(counts, 1.0)[None, None, :, :]
    return next_grid


def solution(mesh):
    placed = (P(("band", "row"), None), P(("band", "row")), P(("band", "row")), P("band"))
    return jax.shard_map(
        local,
        mesh=mesh,
        in_specs=placed,
        out_specs=P(("band", "row"), None, None, None),
        check_vma=False,
    )
```

profile of v0, /device:TPU:44, one launch (start us, length us, event | category | flops | bytes accessed | tf_op | source)
XLA Modules:
  0.0 156.9 jit_solution(13117734031525655496)
XLA Ops:
  0.0 0.7 broadcast_add_fusion
  0.7 0.7 convert.18
  1.4 0.7 convert.19
  2.0 8.6 %multiply_convert_fusion.1 = (bf16[4096,128]{1,0:T(8,128)(2,1)S(1)}, bf16[4096,128]{1,0:T(8,128)(2,1)S(1)}) fusion(s32[128]{0:T(128)S(1)} %broadcast_add_fusion), kind=kLoop, calls=%fused_computation.24 | loop fusion | flops 9961472 | bytes 2097664 | tf_op jit(solution)/shard_map/convert.6
  10.7 3.5 %fusion.23 = bf16[256,512]{1,0:T(8,128)(2,1)S(1)} fusion(bf16[512,4096]{1,0:T(8,128)(2,1)} %param.4, bf16[4096,128]{1,0:T(8,128)(2,1)S(1)} %get-tuple-element.8, bf16[4096,128]{1,0:T(8,128)(2,1)S(1)} %get-tuple-element.7), kind=kOutput, calls=%fused_computation.28 | convolution fusion | flops 1078067200 | bytes 6553600 | tf_op jit(solution)/shard_map/dot_general | solution.py:24
  14.2 0.3 copy.10
  14.5 0.1 broadcast_in_dim.2
  14.6 0.5 pad_maximum_fusion
  15.2 98.3 %all_to_all.18 = bf16[512,4,128]{0,1,2:T(4,128)(2,1)S(1)} all-to-all(bf16[512,4,128]{0,1,2:T(4,128)(2,1)S(1)} %pad_maximum_fusion), channel_id=1, replica_groups=mesh['band'=4,'row'=64] {'row'}, dimensions={2} | all-to-all | bytes 1048576 | tf_op jit(solution)/shard_map/all_to_all | solution.py:31
  113.4 0.2 copy.16
  113.6 0.4 all_to_all.16
  114.0 0.0 copy-start
  114.0 0.2 slice_convert_fusion.1
  114.2 2.2 %iota_compare_fusion.8 = pred[32768,128]{0,1:T(32,128)(4,1)S(1)} fusion(f32[32768]{0:T(1024)S(1)} %bitcast.37), kind=kLoop, calls=%fused_computation.6.clone.clone.clone.clone.2 | loop fusion | flops 4194304 | bytes 4325376 | tf_op jit(solution)/shard_map/ts,tr->sr/dot_general | solution.py:37
  116.4 4.9 %fusion.6 = bf16[32768,128]{0,1:T(8,128)(2,1)} fusion(f32[32768]{0:T(1024)S(1)} %bitcast.38), kind=kLoop, calls=%fused_computation.8 | loop fusion | flops 8388608 | bytes 8519680 | tf_op jit(solution)/shard_map/convert_element_type | solution.py:36
  121.3 0.0 copy-done
  121.3 14.4 %fusion.50 = pred[32768,128,1,1]{1,0,3,2:T(32,128)(4,1)} fusion(f32[32768]{0:T(1024)S(1)} %bitcast.39), kind=kLoop, calls=%fused_computation.4.clone.clone.clone.clone.clone.clone.2 | loop fusion | flops 4194304 | bytes 4325376 | tf_op jit(solution)/shard_map/ts,tcfr->fcsr/dot_general | solution.py:39
  135.7 0.0 slice-start
  135.7 7.1 %fusion.36 = f32[128,128]{1,0:T(8,128)S(1)} fusion(f32[32768]{0:T(1024)S(1)} %bitcast.40, pred[32768,128]{0,1:T(32,128)(4,1)S(1)} %iota_compare_fusion.8), kind=kOutput, calls=%fused_computation.31 | convolution fusion | flops 1082146816 | bytes 4390912 | tf_op jit(solution)/shard_map/ts,tr->sr/dot_general | solution.py:37
  142.8 0.1 copy.12
  142.9 0.0 slice-done
  143.0 13.1 %fusion.31 = f32[2,2,128,128]{2,3,0,1:T(8,128)S(1)} fusion(bf16[32768,128]{0,1:T(8,128)(2,1)} %fusion.6, bf16[32768,2,2]{0,2,1:T(2,128)(2,1)S(1)} %slice-done, f32[128,128]{0,1:T(8,128)S(1)} %copy.12, pred[32768,128,1,1]{1,0,3,2:T(32,128)(4,1)} %fusion.50), kind=kOutput, calls=%fused_computation.30 | convolution fusion | flops 4311810048 | bytes 13172736 | tf_op jit(solution)/shard_map/ts,tcfr->fcsr/dot_general | solution.py:39
  156.1 0.8 copy.13
  (3 shorter events, 0.0 us)
Async XLA Ops:
  114.0 7.3 %copy-start = (bf16[32768,4,2]{0,2,1:T(2,128)(2,1)}, bf16[32768,4,2]{0,2,1:T(2,128)(2,1)S(1)}, u32[]{:S(2)}) copy-start(bf16[32768,4,2]{0,2,1:T(2,128)(2,1)S(1)} %all_to_all.16) | copy-start | bytes 1572868
  135.7 7.2 %slice-start = ((bf16[32768,4,2]{0,2,1:T(2,128)(2,1)}), bf16[32768,2,2]{0,2,1:T(2,128)(2,1)S(1)}, s32[]{:S(2)}) async-start(bf16[32768,4,2]{0,2,1:T(2,128)(2,1)} %copy-done), calls=%async_computation.1 | async-start | bytes 524288 | tf_op jit(solution)/shard_map/slice | solution.py:32
where the time goes:
time: 157 us
  blocking collectives  98.3 us (63%)
  other arithmetic  32.9 us (21%)
  matrix products  23.7 us (15%)
  local copies, waits for them, and re-layouts  1.89 us (1%)
    all_to_all x1, blocking collectives, local(): lax.all_to_all(packed, 'row', split_axis=2, concat_axis=0, tiled=True)  98.3 us
    dot_general x1, other arithmetic, local(): jnp.einsum('ts,tcfr->fcsr', source_hot, weighted, preferred_element_type=...  14.4 us
    dot_general x1, matrix products, local(): jnp.einsum('ts,tcfr->fcsr', source_hot, weighted, preferred_element_type=...  13.1 us
    another operation x3, other arithmetic  10 us
    dot_general x1, matrix products, local(): jnp.einsum('ts,tr->sr', source_hot, receiver_hot, preferred_element_type=...  7.14 us
    convert_element_type x1, other arithmetic, local(): (receiver_value[:, None] == receiver_range[None, :]).astype(jnp.bfloat16)  4.92 us
    dot_general x1, matrix products, local(): jnp.dot(shot_traces, table, preferred_element_type=jnp.float32)  3.48 us

commit v1 on v0

--- a/solution.py
+++ b/solution.py
@@ -28,7 +28,10 @@
     cells = jnp.stack([source_cell, receiver_cell], axis=1).astype(jnp.bfloat16)
     cells = jnp.broadcast_to(cells[:, :, None], (local_traces, 2, band_size))
     packed = jnp.concatenate([spectra, cells], axis=1)
-    moved = lax.all_to_all(packed, "row", split_axis=2, concat_axis=0, tiled=True)
+    moved = jnp.concatenate(
+        lax.all_to_all(jnp.stack(jnp.split(packed, lax.axis_size("row"), axis=2)), "row", 0, 0),
+        axis=0,
+    )
     received = moved[:, 0:2, :]
     source_value = moved[:, 2, 0].astype(jnp.float32)
     receiver_value = moved[:, 3, 0].astype(jnp.float32)

time: 157 us -> 158 us (level)
    another operation x3 -> x4, other arithmetic: 10 us -> 10 us
where the time goes in v1:
time: 158 us
  blocking collectives  98.3 us (62%)
  other arithmetic  33.7 us (21%)
  matrix products  23.7 us (15%)
  local copies, waits for them, and re-layouts  1.89 us (1%)
    all_to_all x1, blocking collectives, local(): lax.all_to_all(jnp.stack(jnp.split(packed, lax.axis_size('row'), axis=2))...  98.3 us
    dot_general x1, other arithmetic, local(): jnp.einsum('ts,tcfr->fcsr', source_hot, weighted, preferred_element_type=...  14.4 us
    dot_general x1, matrix products, local(): jnp.einsum('ts,tcfr->fcsr', source_hot, weighted, preferred_element_type=...  13.1 us
    another operation x3, other arithmetic  10 us
    dot_general x1, matrix products, local(): jnp.einsum('ts,tr->sr', source_hot, receiver_hot, preferred_element_type=...  7.13 us
    convert_element_type x1, other arithmetic, local(): (receiver_value[:, None] == receiver_range[None, :]).astype(jnp.bfloat16)  4.92 us
    dot_general x1, matrix products, local(): jnp.dot(shot_traces, table, preferred_element_type=jnp.float32)  3.48 us

profile of v1, /device:TPU:44, one launch (start us, length us, event | category | flops | bytes accessed | tf_op | source)
XLA Modules:
  0.0 157.9 jit_solution(200582019703976962)
XLA Ops:
  0.0 0.7 broadcast_add_fusion
  0.7 0.7 convert.18
  1.4 0.7 convert.19
  2.0 8.6 %multiply_convert_fusion.1 = (bf16[4096,128]{1,0:T(8,128)(2,1)S(1)}, bf16[4096,128]{1,0:T(8,128)(2,1)S(1)}) fusion(s32[128]{0:T(128)S(1)} %broadcast_add_fusion), kind=kLoop, calls=%fused_computation.87 | loop fusion | flops 9961472 | bytes 2097664 | tf_op jit(solution)/shard_map/convert.6
  10.7 3.5 %fusion.23 = bf16[256,512]{1,0:T(8,128)(2,1)S(1)} fusion(bf16[512,4096]{1,0:T(8,128)(2,1)} %param.4, bf16[4096,128]{1,0:T(8,128)(2,1)S(1)} %get-tuple-element.8, bf16[4096,128]{1,0:T(8,128)(2,1)S(1)} %get-tuple-element.7), kind=kOutput, calls=%fused_computation.91 | convolution fusion | flops 1078067200 | bytes 6553600 | tf_op jit(solution)/shard_map/dot_general | solution.py:24
  14.2 0.3 copy.72
  14.5 0.1 broadcast_in_dim.2
  16.2 98.3 %all_to_all.5 = bf16[64,512,4,2]{1,2,3,0:T(4,128)(2,1)S(1)} all-to-all(bf16[64,512,4,2]{1,2,3,0:T(4,128)(2,1)S(1)} %constant_dynamic-update-slice_fusion), channel_id=1, replica_groups=mesh['band'=4,'row'=64] {'row'}, dimensions={0} | all-to-all | bytes 1048576 | tf_op jit(solution)/shard_map/all_to_all | solution.py:32
  114.4 0.2 copy.73
  114.6 0.4 reshape.61
  115.0 0.0 copy-start
  115.0 0.2 slice_convert_fusion.1
  115.2 2.2 %iota_compare_fusion.8 = pred[32768,128]{0,1:T(32,128)(4,1)S(1)} fusion(f32[32768]{0:T(1024)S(1)} %bitcast.287), kind=kLoop, calls=%fused_computation.6.clone.clone.clone.clone.2 | loop fusion | flops 4194304 | bytes 4325376 | tf_op jit(solution)/shard_map/ts,tr->sr/dot_general | solution.py:40
  117.4 4.9 %fusion.6 = bf16[32768,128]{0,1:T(8,128)(2,1)} fusion(f32[32768]{0:T(1024)S(1)} %bitcast.288), kind=kLoop, calls=%fused_computation.8 | loop fusion | flops 8388608 | bytes 8519680 | tf_op jit(solution)/shard_map/convert_element_type | solution.py:39
  122.3 0.0 copy-done
  122.3 14.4 %fusion.177 = pred[32768,128,1,1]{1,0,3,2:T(32,128)(4,1)} fusion(f32[32768]{0:T(1024)S(1)} %bitcast.289), kind=kLoop, calls=%fused_computation.4.clone.clone.clone.clone.clone.clone.2 | loop fusion | flops 4194304 | bytes 4325376 | tf_op jit(solution)/shard_map/ts,tcfr->fcsr/dot_general | solution.py:42
  136.7 0.0 slice-start
  136.7 7.1 %fusion.36 = f32[128,128]{1,0:T(8,128)S(1)} fusion(f32[32768]{0:T(1024)S(1)} %bitcast.290, pred[32768,128]{0,1:T(32,128)(4,1)S(1)} %iota_compare_fusion.8), kind=kOutput, calls=%fused_computation.94 | convolution fusion | flops 1082146816 | bytes 4390912 | tf_op jit(solution)/shard_map/ts,tr->sr/dot_general | solution.py:40
  143.8 0.1 copy.74
  143.9 0.0 slice-done
  143.9 13.1 %fusion.31 = f32[2,2,128,128]{2,3,0,1:T(8,128)S(1)} fusion(bf16[32768,128]{0,1:T(8,128)(2,1)} %fusion.6, bf16[32768,2,2]{0,2,1:T(2,128)(2,1)S(1)} %slice-done, f32[128,128]{0,1:T(8,128)S(1)} %copy.74, pred[32768,128,1,1]{1,0,3,2:T(32,128)(4,1)} %fusion.177), kind=kOutput, calls=%fused_computation.93 | convolution fusion | flops 4311810048 | bytes 13172736 | tf_op jit(solution)/shard_map/ts,tcfr->fcsr/dot_general | solution.py:42
  157.0 0.8 copy.75
  (67 shorter events, 1.4 us)
Async XLA Ops:
  115.0 7.3 %copy-start = (bf16[32768,4,2]{0,2,1:T(2,128)(2,1)}, bf16[32768,4,2]{0,2,1:T(2,128)(2,1)S(1)}, u32[]{:S(2)}) copy-start(bf16[32768,4,2]{0,2,1:T(2,128)(2,1)S(1)} %reshape.61) | copy-start | bytes 1572868
  136.7 7.2 %slice-start = ((bf16[32768,4,2]{0,2,1:T(2,128)(2,1)}), bf16[32768,2,2]{0,2,1:T(2,128)(2,1)S(1)}, s32[]{:S(2)}) async-start(bf16[32768,4,2]{0,2,1:T(2,128)(2,1)} %copy-done), calls=%async_computation.1 | async-start | bytes 524288 | tf_op jit(solution)/shard_map/slice | solution.py:35
